TPU v7x, 32 devices: a whole 2x2x4 slice. The times are simulated.
32 devices in a mesh: seq: 8 (over y, x, core), tp: 4 (over z).
Axes of the slice: x: 2, y: 2, z: 4, core: 2. Of those that a mesh axis runs over, the one named last changes fastest.
Arguments:
- tokens: bfloat16 [4096, 3584], P('seq'), may hold values from -6 to 6
- norm_gain: float32 [3584], replicated, may hold values from 0.5 to 1.5
- q_weight: bfloat16 [3584, 3584], P(None, 'tp'), may hold values from -0.09375 to 0.09375
- q_bias: float32 [3584], P('tp'), may hold values from -9 to 9
- k_weight: bfloat16 [3584, 512], P(None, 'tp'), may hold values from -0.09375 to 0.09375
- k_bias: float32 [512], P('tp'), may hold values from -9 to 9
- v_weight: bfloat16 [3584, 512], P(None, 'tp'), may hold values from -0.09375 to 0.09375
- v_bias: float32 [512], P('tp'), may hold values from -5 to 5
- o_weight: bfloat16 [3584, 3584], P('tp'), may hold values from -0.09375 to 0.09375
- doc_ids: int32 [4096], replicated, may hold values from 0 to 7, never falling along the last dimension, each value on 1 to 2560 neighbouring positions
Outputs:
- attn_out: bfloat16 [4096, 3584], P('seq', 'tp')
Inputs may be any that keep to these rules, and one draw needn't show every extreme that they name: `doc_ids`: document numbers never fall along the sequence; each document holds 1 to 2560 tokens and one holds exactly that many.
All inputs are finite; a program needn't handle non-finite values.
Results may differ from a plain program's by a relative error of at most 0.012.
Values may be sent and summed in bfloat16 or wider, within the bound.
A program may use at most 128 MiB of HBM per device.

v0:
```python
import functools
import math

import jax
import jax.numpy as jnp
import numpy as np
from jax import lax
from jax.experimental import pallas as pl
from jax.experimental.pallas import tpu as pltpu
from jax.sharding import PartitionSpec as P

HD = 128
MESH = pl.DeviceIdType.MESH
rope_base = 1000000.0
VMEM = pltpu.VMEM
LAG = 1


def rope_tables(rows, blocks):
    half = HD // 2
    inv = rope_base ** (-(np.arange(half, dtype=np.float64) * 2.0) / HD)
    inv = np.concatenate([inv, inv])[None, :]
    near = np.arange(rows)[:, None] * inv
    far = np.arange(blocks)[:, None] * rows * inv
    near = np.stack([np.cos(near), np.sin(near)]).astype(np.float32)
    far = np.stack([np.cos(far), np.sin(far)])[:, :, None, :].astype(np.float32)
    return near, far


def attend(
    seq_count, tp_count, reach, chunk,
    tokens_hbm, gain_ref, wq_hbm, qb_ref, wk_hbm, kb_ref, wv_hbm, vb_ref, wo_hbm,
    kdoc_ref, near_hbm, far_ref, out_ref,
    tokens, normed, wq, wkv, wo, near, q_ref, kv_ref, kv_in, sent, got, own,
    load_sems, kv_send, kv_pass, kv_recv, send_sem, recv_sem,
):
    place = lax.axis_index("seq")
    turn = lax.axis_index("tp")
    rows, width = q_ref.shape
    heads = width // HD
    cols = out_ref.shape[1]
    parts = rows // chunk
    step = 2 * HD
    spans = [(lo, min(step, width - lo)) for lo in range(0, width, step)]
    loads = [
        pltpu.make_async_copy(tokens_hbm, tokens, load_sems.at[0]),
        pltpu.make_async_copy(wk_hbm, wkv.at[:, pl.ds(0, HD)], load_sems.at[1]),
        pltpu.make_async_copy(wv_hbm, wkv.at[:, pl.ds(HD, HD)], load_sems.at[2]),
        pltpu.make_async_copy(near_hbm, near, load_sems.at[3]),
    ]
    for index, (lo, size) in enumerate(spans):
        cut = pl.ds(lo, size)
        loads.append(
            pltpu.make_async_copy(wq_hbm.at[:, cut], wq.at[:, cut], load_sems.at[4 + index])
        )
    load = pltpu.make_async_copy(wo_hbm, wo, load_sems.at[4 + len(spans)])
    loads.append(load)
    for copy in loads:
        copy.start()

    barrier = pltpu.get_barrier_semaphore()
    span = min(reach + 1, seq_count - 1)
    for away in range(1, span + 1):
        @pl.when(place >= away)
        def _():
            pl.semaphore_signal(barrier, inc=1, device_id={"seq": place - away}, device_id_type=MESH)

        @pl.when(place + away < seq_count)
        def _():
            pl.semaphore_signal(barrier, inc=1, device_id={"seq": place + away}, device_id_type=MESH)

    @pl.when(turn > 0)
    def _():
        pl.semaphore_signal(barrier, inc=1, device_id={"tp": turn - 1}, device_id_type=MESH)

    @pl.when(turn < tp_count - 1)
    def _():
        pl.semaphore_signal(barrier, inc=1, device_id={"tp": turn + 1}, device_id_type=MESH)

    behind = jnp.minimum(place, reach)
    near_count = jnp.minimum(place, span) + jnp.minimum(seq_count - 1 - place, span)
    sides = jnp.where(turn > 0, 1, 0) + jnp.where(turn < tp_count - 1, 1, 0)

    loads[0].wait()
    slab = 64
    gain = gain_ref[...].reshape(1, gain_ref.shape[0])

    @pl.loop(0, rows // slab)
    def _(index):
        cut = pl.ds(pl.multiple_of(index * slab, slab), slab)
        wide = tokens[cut, :].astype(jnp.float32)
        mean = jnp.mean(wide * wide, axis=-1, keepdims=True)
        normed[cut, :] = (wide * lax.rsqrt(mean + 1e-06) * gain).astype(jnp.bfloat16)

    loads[3].wait()
    far_cos, far_sin = far_ref[0, place], far_ref[1, place]
    cos = near[0] * far_cos - near[1] * far_sin
    sin = near[1] * far_cos + near[0] * far_sin
    lane = lax.broadcasted_iota(jnp.int32, (rows, HD), 1)
    near[0] = cos
    near[1] = jnp.where(lane < HD // 2, -sin, sin)

    def rope(t):
        return (t * near[0] + pltpu.roll(t, HD // 2, 1) * near[1]).astype(jnp.bfloat16)

    loads[1].wait()
    loads[2].wait()
    kv = jnp.dot(normed[...], wkv[...], preferred_element_type=jnp.float32)
    kv_ref[0] = rope(kv[:, :HD] + kb_ref[...].reshape(1, HD))
    kv_ref[1] = (kv[:, HD:] + vb_ref[...].reshape(1, HD)).astype(jnp.bfloat16)

    pl.semaphore_wait(barrier, near_count + sides)

    odd = lax.rem(place, 2) == 1
    partner = place + 1 - 2 * lax.rem(place, 2)

    def kv_copy(away):
        return pltpu.make_async_remote_copy(
            src_ref=kv_ref, dst_ref=kv_in.at[away - 1],
            send_sem=kv_send.at[away - 1], recv_sem=kv_recv.at[away - 1],
            device_id={"seq": lax.rem(place + away, seq_count)}, device_id_type=MESH,
        )

    def relay(away, landing):
        return pltpu.make_async_remote_copy(
            src_ref=kv_in.at[away - 1], dst_ref=kv_in.at[landing - 1],
            send_sem=kv_pass.at[away - 1], recv_sem=kv_recv.at[landing - 1],
            device_id={"seq": partner}, device_id_type=MESH,
        )

    evens = [away for away in range(2, reach + 2, 2) if away < seq_count]

    def wanted(away):
        return odd if away > reach else (place >= 0)

    def each_send(act):
        for away in evens:
            @pl.when((place + away < seq_count) & wanted(away))
            def _():
                act(kv_copy(away))

        @pl.when(jnp.logical_not(odd))
        def _():
            act(kv_copy(1))

    def each_relay(act):
        for away in evens:
            if away + 1 <= reach:
                @pl.when((place >= away) & jnp.logical_not(odd))
                def _():
                    act(relay(away, away + 1))

            @pl.when((place >= away) & odd)
            def _():
                act(relay(away, away - 1))

    each_send(lambda copy: copy.start())

    for index, (lo, size) in enumerate(spans):
        loads[4 + index].wait()
        out = jnp.dot(
            normed[...], wq[:, lo:lo + size], preferred_element_type=jnp.float32
        ) + qb_ref[lo:lo + size].reshape(1, size)
        for head in range(0, size, HD):
            q_ref[:, lo + head:lo + head + HD] = rope(out[:, head:head + HD])

    for away in evens:
        @pl.when((place >= away) & wanted(away))
        def _():
            kv_copy(away).wait_recv()

        if away + 1 <= reach:
            @pl.when((place >= away) & jnp.logical_not(odd))
            def _():
                relay(away, away + 1).start()

        @pl.when((place >= away) & odd)
        def _():
            relay(away, away - 1).start()

    def term_copy(side, dest, part):
        cut = pl.ds(pl.multiple_of(part * chunk, chunk), chunk)
        target = lax.rem(turn + (1 if side == 0 else tp_count - 1), tp_count)
        return pltpu.make_async_remote_copy(
            src_ref=sent.at[dest, cut], dst_ref=got.at[side, dest, cut],
            send_sem=send_sem.at[dest, part], recv_sem=recv_sem.at[side, dest, part],
            device_id={"tp": target}, device_id_type=MESH,
        )

    factor = math.log2(math.e) / HD**0.5
    order = sorted(range(tp_count), key=lambda d: (-abs(2 * d - tp_count + 1), -d))

    def forward(part, first):
        cut = pl.ds(pl.multiple_of(part * chunk, chunk), chunk)
        for side in (0, 1):
            chosen = (2 * turn < tp_count) if (side == 0) == first else (2 * turn >= tp_count)
            for dest in order:
                inner = (turn > 0) & (dest > turn) if side == 0 else (
                    (turn < tp_count - 1) & (dest < turn))

                @pl.when(inner & chosen)
                def _():
                    term_copy(side, dest, part).wait_recv()
                    sent[dest, cut] = (
                        sent[dest, cut].astype(jnp.float32) + got[side, dest, cut].astype(jnp.float32)
                    ).astype(jnp.bfloat16)
                    term_copy(side, dest, part).start()

    def finish(part):
        cut = pl.ds(pl.multiple_of(part * chunk, chunk), chunk)
        for dest in range(tp_count):
            for side in (0, 1):
                edge = (turn > 0) if side == 0 else (turn < tp_count - 1)

                @pl.when((dest == turn) & edge)
                def _():
                    term_copy(side, dest, part).wait_recv()
                    own[cut, :] = own[cut, :] + got[side, dest, cut].astype(jnp.float32)

        out_ref[cut, :] = own[cut, :].astype(jnp.bfloat16)

    def piece(part):
        cut = pl.ds(pl.multiple_of(part * chunk, chunk), chunk)
        q = jnp.concatenate([q_ref[cut, h * HD:(h + 1) * HD] for h in range(heads)], axis=0)
        lanes = kdoc_ref[place, :, cut].astype(jnp.float32)
        qdoc = jnp.broadcast_to(lanes, (chunk, chunk)).T[:, :1]

        def block(state, k, v, visible):
            top, total, summed = state
            s = lax.dot_general(q, k, (((1,), (1,)), ((), ())), preferred_element_type=jnp.float32)
            s = s.reshape(heads, chunk, rows) * factor
            s = jnp.where(visible[None], s, -1e30)
            fresh = jnp.maximum(top, jnp.max(s, axis=-1, keepdims=True))
            e = jnp.exp2(s - fresh)
            scale = jnp.exp2(top - fresh)
            total = total * scale + jnp.sum(e, axis=-1, keepdims=True)
            pv = jnp.dot(
                e.astype(jnp.bfloat16).reshape(heads * chunk, rows), v,
                preferred_element_type=jnp.float32,
            )
            return fresh, total, summed * scale + pv.reshape(heads, chunk, HD)

        row = part * chunk + lax.broadcasted_iota(jnp.int32, (chunk, rows), 0)
        col = lax.broadcasted_iota(jnp.int32, (chunk, rows), 1)
        state = (
            jnp.full((heads, chunk, 1), -1e30, jnp.float32),
            jnp.zeros((heads, chunk, 1), jnp.float32),
            jnp.zeros((heads, chunk, HD), jnp.float32),
        )
        state = block(
            state, kv_ref[0], kv_ref[1], (col <= row) & (qdoc == kdoc_ref[place].astype(jnp.float32))
        )

        def earlier(away, state):
            @pl.when((part == 0) & (lax.rem(away, 2) == 1))
            def _():
                kv_copy(away).wait_recv()

            return block(
                state, kv_in[away - 1, 0], kv_in[away - 1, 1],
                qdoc == kdoc_ref[place - away].astype(jnp.float32),
            )

        _, total, summed = lax.fori_loop(1, behind + 1, earlier, state)
        context = (summed / total).astype(jnp.bfloat16)
        context = jnp.concatenate([context[h] for h in range(heads)], axis=1)

        @pl.when(part == 0)
        def _():
            load.wait()

        for dest in order:
            term = jnp.dot(
                context, wo[:, dest * cols:(dest + 1) * cols], preferred_element_type=jnp.float32
            )

            @pl.when(dest == turn)
            def _():
                own[cut, :] = term

            @pl.when(dest != turn)
            def _():
                sent[dest, cut] = term.astype(jnp.bfloat16)

            @pl.when((turn == 0) & (dest > 0))
            def _():
                term_copy(0, dest, part).start()

            @pl.when((turn == tp_count - 1) & (dest < tp_count - 1))
            def _():
                term_copy(1, dest, part).start()

    @pl.loop(0, parts + LAG + 1)
    def _(part):
        @pl.when(part < parts)
        def _():
            piece(part)

        @pl.when((part >= LAG) & (part < parts + LAG))
        def _():
            forward(part - LAG, True)

        @pl.when(part >= LAG + 1)
        def _():
            forward(part - LAG - 1, False)

    @pl.loop(0, parts)
    def _(part):
        finish(part)

    @pl.loop(0, parts)
    def _(part):
        for dest in range(tp_count):
            @pl.when(dest != turn)
            def _():
                term_copy(0, dest, part).wait_send()

    each_send(lambda copy: copy.wait_send())
    each_relay(lambda copy: copy.wait_send())


def body(
    tokens, norm_gain, q_weight, q_bias, k_weight, k_bias, v_weight, v_bias, o_weight, doc_ids
):
    rows, model = tokens.shape
    seq_count = lax.axis_size("seq")
    tp_count = lax.axis_size("tp")
    width = q_weight.shape[1]
    cols = o_weight.shape[1] // tp_count
    reach = min(seq_count - 1, (seq_count * rows // 2 + 2 * rows - 2) // rows)
    chunk = rows // 4
    parts = rows // chunk
    near, far = rope_tables(rows, seq_count)
    hbm = pl.BlockSpec(memory_space=pl.ANY)
    vmem = pl.BlockSpec(memory_space=VMEM)
    slots = reach + 1
    spans = -(-width // (2 * HD))
    kdoc = doc_ids.reshape(seq_count, 1, rows)
    return pl.pallas_call(
        functools.partial(attend, seq_count, tp_count, reach, chunk),
        out_shape=jax.ShapeDtypeStruct((rows, cols), jnp.bfloat16),
        in_specs=[hbm, vmem, hbm, vmem, hbm, vmem, hbm, vmem, hbm, vmem, hbm, vmem],
        out_specs=vmem,
        scratch_shapes=[
            VMEM((rows, model), jnp.bfloat16),
            VMEM((rows, model), jnp.bfloat16),
            VMEM((model, width), jnp.bfloat16),
            VMEM((model, 2 * HD), jnp.bfloat16),
            VMEM(o_weight.shape, jnp.bfloat16),
            VMEM((2, rows, HD), jnp.float32),
            VMEM((rows, width), jnp.bfloat16),
            VMEM((2, rows, HD), jnp.bfloat16),
            VMEM((slots, 2, rows, HD), jnp.bfloat16),
            VMEM((tp_count, rows, cols), jnp.bfloat16),
            VMEM((2, tp_count, rows, cols), jnp.bfloat16),
            VMEM((rows, cols), jnp.float32),
            pltpu.SemaphoreType.DMA((5 + spans,)),
            pltpu.SemaphoreType.DMA((slots,)),
            pltpu.SemaphoreType.DMA((slots,)),
            pltpu.SemaphoreType.DMA((slots,)),
            pltpu.SemaphoreType.DMA((tp_count, parts)),
            pltpu.SemaphoreType.DMA((2, tp_count, parts)),
        ],
        compiler_params=pltpu.CompilerParams(
            collective_id=0, has_side_effects=True, vmem_limit_bytes=56 * 1024 * 1024
        ),
    )(
        tokens, norm_gain, q_weight, q_bias, k_weight, k_bias, v_weight, v_bias, o_weight,
        kdoc, jnp.asarray(near), jnp.asarray(far),
    )


def solution(mesh):
    placed = (
        P("seq", None),
        P(),
        P(None, "tp"),
        P("tp"),
        P(None, "tp"),
        P("tp"),
        P(None, "tp"),
        P("tp"),
        P("tp", None),
        P(),
    )
    return jax.shard_map(
        body, mesh=mesh, in_specs=placed, out_specs=P("seq", "tp"), check_vma=False
    )
```

profile of v0, /device:TPU:28, one launch (start us, length us, event | category | flops | bytes accessed | tf_op | source)
XLA Modules:
  0.0 101.3 jit_solution(16055225733313562510)
XLA Ops:
  0.0 99.1 %shard_map.118 = bf16[512,896]{1,0:T(8,128)(2,1)} custom-call(bf16[512,3584]{1,0:T(8,128)(2,1)} %tokens_hbm.1, f32[3584]{0:T(1024)} %gain_ref.1, bf16[3584,896]{1,0:T(8,128)(2,1)} %wq_hbm.1, f32[896]{0:T(1024)} %qb_ref.1, bf16[3584,128]{1,0:T(8,128)(2,1)} %wk_hbm.1, f32[128]{0:T(128)} %kb_ref.1, bf16[3584,128]{1,0:T(8,128)(2,1)} %wv_hbm.1, f32[128]{0:T(128)} %vb_ref.1, ...), custom_call_target="tpu_custom_call" | custom-call | tf_op jit(solution)/shard_map/pallas_call | solution.py:339
  99.1 2.2 %copy.14 = bf16[512,896]{1,0:T(8,128)(2,1)} copy(bf16[512,896]{1,0:T(8,128)(2,1)} %shard_map.118) | data formatting | bytes 1835008
where the time goes:
time: 101 us
  Pallas kernels  99.1 us (98%)
  local copies, waits for them, and re-layouts  2.18 us (2%)
    pallas_call x1, Pallas kernels, body(): pl.pallas_call(functools.partial(attend, seq_count, tp_count, reach, chun...  99.1 us
    unnamed x1, local copies, waits for them, and re-layouts  2.18 us

commit v1 on v0

--- a/solution.py
+++ b/solution.py
@@ -14,6 +14,8 @@
 rope_base = 1000000.0
 VMEM = pltpu.VMEM
 LAG = 1
+AHEAD = 3
+BACK = 1
 
 
 def rope_tables(rows, blocks):
@@ -31,31 +33,39 @@
     seq_count, tp_count, reach, chunk,
     tokens_hbm, gain_ref, wq_hbm, qb_ref, wk_hbm, kb_ref, wv_hbm, vb_ref, wo_hbm,
     kdoc_ref, near_hbm, far_ref, out_ref,
-    tokens, normed, wq, wkv, wo, near, q_ref, kv_ref, kv_in, sent, got, own,
+    tokens, normed, wq, wkv, wo, near, q_ref, kv_ref, kv_in, kext, acc, tops, totals, sent, got,
     load_sems, kv_send, kv_pass, kv_recv, send_sem, recv_sem,
 ):
     place = lax.axis_index("seq")
     turn = lax.axis_index("tp")
-    rows, width = q_ref.shape
+    rows, width = tokens.shape[0], wq.shape[1]
     heads = width // HD
     cols = out_ref.shape[1]
     parts = rows // chunk
+    factor = math.log2(math.e) / HD**0.5
     step = 2 * HD
     spans = [(lo, min(step, width - lo)) for lo in range(0, width, step)]
-    loads = [
-        pltpu.make_async_copy(tokens_hbm, tokens, load_sems.at[0]),
-        pltpu.make_async_copy(wk_hbm, wkv.at[:, pl.ds(0, HD)], load_sems.at[1]),
-        pltpu.make_async_copy(wv_hbm, wkv.at[:, pl.ds(HD, HD)], load_sems.at[2]),
-        pltpu.make_async_copy(near_hbm, near, load_sems.at[3]),
+    slab = rows // 4
+    token_loads = [
+        pltpu.make_async_copy(
+            tokens_hbm.at[pl.ds(index * slab, slab)], tokens.at[pl.ds(index * slab, slab)],
+            load_sems.at[index],
+        )
+        for index in range(4)
     ]
-    for index, (lo, size) in enumerate(spans):
-        cut = pl.ds(lo, size)
-        loads.append(
-            pltpu.make_async_copy(wq_hbm.at[:, cut], wq.at[:, cut], load_sems.at[4 + index])
-        )
-    load = pltpu.make_async_copy(wo_hbm, wo, load_sems.at[4 + len(spans)])
-    loads.append(load)
-    for copy in loads:
+    near_load = pltpu.make_async_copy(near_hbm, near, load_sems.at[4])
+    kv_loads = [
+        pltpu.make_async_copy(wk_hbm, wkv.at[:, pl.ds(0, HD)], load_sems.at[5]),
+        pltpu.make_async_copy(wv_hbm, wkv.at[:, pl.ds(HD, HD)], load_sems.at[6]),
+    ]
+    q_loads = [
+        pltpu.make_async_copy(
+            wq_hbm.at[:, pl.ds(lo, size)], wq.at[:, pl.ds(lo, size)], load_sems.at[7 + index]
+        )
+        for index, (lo, size) in enumerate(spans)
+    ]
+    load = pltpu.make_async_copy(wo_hbm, wo, load_sems.at[7 + len(spans)])
+    for copy in token_loads + kv_loads + [near_load]:
         copy.start()
 
     barrier = pltpu.get_barrier_semaphore()
@@ -81,33 +91,47 @@
     near_count = jnp.minimum(place, span) + jnp.minimum(seq_count - 1 - place, span)
     sides = jnp.where(turn > 0, 1, 0) + jnp.where(turn < tp_count - 1, 1, 0)
 
-    loads[0].wait()
-    slab = 64
+    lane = lax.broadcasted_iota(jnp.int32, (rows, HD), 1)
+    doc = lax.broadcasted_iota(jnp.int32, (HD, rows), 0)
+    for away in range(reach + 1):
+        ids = kdoc_ref[jnp.maximum(place - away, 0)]
+        kext[away] = jnp.where(doc == ids, 1.0, 0.0).T.astype(jnp.bfloat16)
+        if away == 0:
+            veto = jnp.where(doc == ids, 0.0, -1e30).astype(jnp.bfloat16)
+            for part in range(parts):
+                q_ref[part, HD:, :] = jnp.concatenate([veto[:, part * chunk:(part + 1) * chunk]] * heads, axis=1)
+
     gain = gain_ref[...].reshape(1, gain_ref.shape[0])
-
-    @pl.loop(0, rows // slab)
-    def _(index):
-        cut = pl.ds(pl.multiple_of(index * slab, slab), slab)
-        wide = tokens[cut, :].astype(jnp.float32)
-        mean = jnp.mean(wide * wide, axis=-1, keepdims=True)
-        normed[cut, :] = (wide * lax.rsqrt(mean + 1e-06) * gain).astype(jnp.bfloat16)
-
-    loads[3].wait()
+    for index in range(4):
+        token_loads[index].wait()
+        if index == 3:
+            for copy in q_loads:
+                copy.start()
+
+        @pl.loop(0, slab // 64)
+        def _(step):
+            cut = pl.ds(pl.multiple_of(index * slab + step * 64, 64), 64)
+            wide = tokens[cut, :].astype(jnp.float32)
+            mean = jnp.mean(wide * wide, axis=-1, keepdims=True)
+            normed[cut, :] = (wide * lax.rsqrt(mean + 1e-06) * gain).astype(jnp.bfloat16)
+
+    near_load.wait()
     far_cos, far_sin = far_ref[0, place], far_ref[1, place]
     cos = near[0] * far_cos - near[1] * far_sin
     sin = near[1] * far_cos + near[0] * far_sin
-    lane = lax.broadcasted_iota(jnp.int32, (rows, HD), 1)
     near[0] = cos
     near[1] = jnp.where(lane < HD // 2, -sin, sin)
 
     def rope(t):
-        return (t * near[0] + pltpu.roll(t, HD // 2, 1) * near[1]).astype(jnp.bfloat16)
-
-    loads[1].wait()
-    loads[2].wait()
+        return t * near[0] + pltpu.roll(t, HD // 2, 1) * near[1]
+
+    for copy in kv_loads:
+        copy.wait()
     kv = jnp.dot(normed[...], wkv[...], preferred_element_type=jnp.float32)
-    kv_ref[0] = rope(kv[:, :HD] + kb_ref[...].reshape(1, HD))
-    kv_ref[1] = (kv[:, HD:] + vb_ref[...].reshape(1, HD)).astype(jnp.bfloat16)
+    kv_ref[0] = rope(kv[:, :HD] + kb_ref[...].reshape(1, HD)).astype(jnp.bfloat16)
+    values = kv[:, HD:] + vb_ref[...].reshape(1, HD)
+    for lo in range(0, rows, HD):
+        kv_ref[1, lo:lo + HD] = values[lo:lo + HD].T.astype(jnp.bfloat16)
 
     pl.semaphore_wait(barrier, near_count + sides)
 
@@ -157,12 +181,17 @@
     each_send(lambda copy: copy.start())
 
     for index, (lo, size) in enumerate(spans):
-        loads[4 + index].wait()
+        q_loads[index].wait()
+        if index == 1:
+            load.start()
         out = jnp.dot(
             normed[...], wq[:, lo:lo + size], preferred_element_type=jnp.float32
         ) + qb_ref[lo:lo + size].reshape(1, size)
         for head in range(0, size, HD):
-            q_ref[:, lo + head:lo + head + HD] = rope(out[:, head:head + HD])
+            turned = rope(out[:, head:head + HD]) * factor
+            at = (lo + head) // HD * chunk
+            for part in range(parts):
+                q_ref[part, :HD, at:at + chunk] = turned[part * chunk:(part + 1) * chunk].T.astype(jnp.bfloat16)
 
     for away in evens:
         @pl.when((place >= away) & wanted(away))
@@ -187,7 +216,6 @@
             device_id={"tp": target}, device_id_type=MESH,
         )
 
-    factor = math.log2(math.e) / HD**0.5
     order = sorted(range(tp_count), key=lambda d: (-abs(2 * d - tp_count + 1), -d))
 
     def forward(part, first):
@@ -215,73 +243,93 @@
                 @pl.when((dest == turn) & edge)
                 def _():
                     term_copy(side, dest, part).wait_recv()
-                    own[cut, :] = own[cut, :] + got[side, dest, cut].astype(jnp.float32)
-
-        out_ref[cut, :] = own[cut, :].astype(jnp.bfloat16)
+
+            @pl.when(dest == turn)
+            def _():
+                total = sent[dest, cut].astype(jnp.float32)
+                left = jnp.where(turn > 0, got[0, dest, cut].astype(jnp.float32), 0.0)
+                right = jnp.where(turn < tp_count - 1, got[1, dest, cut].astype(jnp.float32), 0.0)
+                out_ref[cut, :] = (total + left + right).astype(jnp.bfloat16)
+
+    wide = step // chunk * chunk
+    tiles = [(lo, min(wide, heads * chunk - lo)) for lo in range(0, heads * chunk, wide)]
 
     def piece(part):
         cut = pl.ds(pl.multiple_of(part * chunk, chunk), chunk)
-        q = jnp.concatenate([q_ref[cut, h * HD:(h + 1) * HD] for h in range(heads)], axis=0)
-        lanes = kdoc_ref[place, :, cut].astype(jnp.float32)
-        qdoc = jnp.broadcast_to(lanes, (chunk, chunk)).T[:, :1]
-
-        def block(state, k, v, visible):
-            top, total, summed = state
-            s = lax.dot_general(q, k, (((1,), (1,)), ((), ())), preferred_element_type=jnp.float32)
-            s = s.reshape(heads, chunk, rows) * factor
-            s = jnp.where(visible[None], s, -1e30)
-            fresh = jnp.maximum(top, jnp.max(s, axis=-1, keepdims=True))
-            e = jnp.exp2(s - fresh)
-            scale = jnp.exp2(top - fresh)
-            total = total * scale + jnp.sum(e, axis=-1, keepdims=True)
-            pv = jnp.dot(
-                e.astype(jnp.bfloat16).reshape(heads * chunk, rows), v,
-                preferred_element_type=jnp.float32,
-            )
-            return fresh, total, summed * scale + pv.reshape(heads, chunk, HD)
-
-        row = part * chunk + lax.broadcasted_iota(jnp.int32, (chunk, rows), 0)
-        col = lax.broadcasted_iota(jnp.int32, (chunk, rows), 1)
-        state = (
-            jnp.full((heads, chunk, 1), -1e30, jnp.float32),
-            jnp.zeros((heads, chunk, 1), jnp.float32),
-            jnp.zeros((heads, chunk, HD), jnp.float32),
-        )
-        state = block(
-            state, kv_ref[0], kv_ref[1], (col <= row) & (qdoc == kdoc_ref[place].astype(jnp.float32))
-        )
-
-        def earlier(away, state):
+        def block(held, away, first):
+            keys = jnp.concatenate([held[0], kext[away]], axis=1)
+            values = jnp.concatenate([held[1, lo:lo + HD] for lo in range(0, rows, HD)], axis=1)
+            if first:
+                key = lax.broadcasted_iota(jnp.int32, (rows, chunk), 0)
+                row = part * chunk + lax.broadcasted_iota(jnp.int32, (rows, chunk), 1)
+                later = jnp.where(key <= row, 0.0, -1e30)
+            def score(tile):
+                lo, size = tile
+                s = jnp.dot(keys, q_ref[part, :, lo:lo + size], preferred_element_type=jnp.float32)
+                if first:
+                    s = s + jnp.concatenate([later] * (size // chunk), axis=1)
+                return s
+
+            def weigh(tile, s):
+                lo, size = tile
+                fresh = jnp.max(s, axis=0, keepdims=True)
+                scale = None
+                if not first:
+                    top = tops[:, lo:lo + size]
+                    fresh = jnp.maximum(top, fresh)
+                    scale = jnp.exp2(top - fresh)
+                e = jnp.exp2(s - fresh)
+                total = jnp.sum(e, axis=0, keepdims=True)
+                if not first:
+                    total = total + totals[:, lo:lo + size] * scale
+                tops[:, lo:lo + size] = fresh
+                totals[:, lo:lo + size] = total
+                return tile, scale, e.astype(jnp.bfloat16)
+
+            def mix(tile, scale, e):
+                return tile, scale, jnp.dot(values, e, preferred_element_type=jnp.float32)
+
+            def gather(tile, scale, pv):
+                lo, size = tile
+                if not first:
+                    pv = pv + acc[:, lo:lo + size] * scale
+                acc[:, lo:lo + size] = pv
+
+            ready = [score(tile) for tile in tiles[:AHEAD]]
+            mixed = []
+            for index, tile in enumerate(tiles):
+                if index + AHEAD < len(tiles):
+                    ready.append(score(tiles[index + AHEAD]))
+                mixed.append(mix(*weigh(tile, ready.pop(0))))
+                if len(mixed) > BACK:
+                    gather(*mixed.pop(0))
+            while mixed:
+                gather(*mixed.pop(0))
+
+        block(kv_ref, 0, True)
+
+        @pl.loop(1, behind + 1)
+        def _(away):
             @pl.when((part == 0) & (lax.rem(away, 2) == 1))
             def _():
                 kv_copy(away).wait_recv()
 
-            return block(
-                state, kv_in[away - 1, 0], kv_in[away - 1, 1],
-                qdoc == kdoc_ref[place - away].astype(jnp.float32),
-            )
-
-        _, total, summed = lax.fori_loop(1, behind + 1, earlier, state)
-        context = (summed / total).astype(jnp.bfloat16)
-        context = jnp.concatenate([context[h] for h in range(heads)], axis=1)
+            block(kv_in.at[away - 1], away, False)
+
+        whole = acc[...] * (1.0 / totals[...])
+        context = jnp.concatenate(
+            [whole[:, h * chunk:(h + 1) * chunk].T.astype(jnp.bfloat16) for h in range(heads)], axis=1
+        )
 
         @pl.when(part == 0)
         def _():
             load.wait()
 
         for dest in order:
-            term = jnp.dot(
+            sent[dest, cut] = jnp.dot(
                 context, wo[:, dest * cols:(dest + 1) * cols], preferred_element_type=jnp.float32
-            )
-
-            @pl.when(dest == turn)
-            def _():
-                own[cut, :] = term
-
-            @pl.when(dest != turn)
-            def _():
-                sent[dest, cut] = term.astype(jnp.bfloat16)
-
+            ).astype(jnp.bfloat16)
+        for dest in order:
             @pl.when((turn == 0) & (dest > 0))
             def _():
                 term_copy(0, dest, part).start()
@@ -328,7 +376,7 @@
     width = q_weight.shape[1]
     cols = o_weight.shape[1] // tp_count
     reach = min(seq_count - 1, (seq_count * rows // 2 + 2 * rows - 2) // rows)
-    chunk = rows // 4
+    chunk = rows // 2
     parts = rows // chunk
     near, far = rope_tables(rows, seq_count)
     hbm = pl.BlockSpec(memory_space=pl.ANY)
@@ -348,13 +396,16 @@
             VMEM((model, 2 * HD), jnp.bfloat16),
             VMEM(o_weight.shape, jnp.bfloat16),
             VMEM((2, rows, HD), jnp.float32),
-            VMEM((rows, width), jnp.bfloat16),
+            VMEM((parts, 2 * HD, width // HD * chunk), jnp.bfloat16),
             VMEM((2, rows, HD), jnp.bfloat16),
             VMEM((slots, 2, rows, HD), jnp.bfloat16),
+            VMEM((slots, rows, HD), jnp.bfloat16),
+            VMEM((HD, width // HD * chunk), jnp.float32),
+            VMEM((1, width // HD * chunk), jnp.float32),
+            VMEM((1, width // HD * chunk), jnp.float32),
             VMEM((tp_count, rows, cols), jnp.bfloat16),
             VMEM((2, tp_count, rows, cols), jnp.bfloat16),
-            VMEM((rows, cols), jnp.float32),
-            pltpu.SemaphoreType.DMA((5 + spans,)),
+            pltpu.SemaphoreType.DMA((8 + spans,)),
             pltpu.SemaphoreType.DMA((slots,)),
             pltpu.SemaphoreType.DMA((slots,)),
             pltpu.SemaphoreType.DMA((slots,)),

time: 101 us -> 113 us (1.12)
  Pallas kernels: 99.1 us -> 111 us
    pallas_call x1, Pallas kernels: 99.1 us -> 111 us  [body(): pl.pallas_call(functools.partial(attend, seq_count, tp_count, reach, chun...]
where the time goes in v1:
time: 113 us
  Pallas kernels  111 us (98%)
  local copies, waits for them, and re-layouts  2.18 us (2%)
    pallas_call x1, Pallas kernels, body(): pl.pallas_call(functools.partial(attend, seq_count, tp_count, reach, chun...  111 us

profile of v1, /device:TPU:28, one launch (start us, length us, event | category | flops | bytes accessed | tf_op | source)
XLA Modules:
  0.0 113.3 jit_solution(1723488978941500903)
XLA Ops:
  0.0 111.1 %shard_map.118 = bf16[512,896]{1,0:T(8,128)(2,1)} custom-call(bf16[512,3584]{1,0:T(8,128)(2,1)} %tokens_hbm.1, f32[3584]{0:T(1024)} %gain_ref.1, bf16[3584,896]{1,0:T(8,128)(2,1)} %wq_hbm.1, f32[896]{0:T(1024)} %qb_ref.1, bf16[3584,128]{1,0:T(8,128)(2,1)} %wk_hbm.1, f32[128]{0:T(128)} %kb_ref.1, bf16[3584,128]{1,0:T(8,128)(2,1)} %wv_hbm.1, f32[128]{0:T(128)} %vb_ref.1, ...), custom_call_target="tpu_custom_call" | custom-call | tf_op jit(solution)/shard_map/pallas_call | solution.py:387
  111.1 2.2 %copy.14 = bf16[512,896]{1,0:T(8,128)(2,1)} copy(bf16[512,896]{1,0:T(8,128)(2,1)} %shard_map.118) | data formatting | bytes 1835008

commit v2 on v1

--- a/solution.py
+++ b/solution.py
@@ -13,7 +13,7 @@
 MESH = pl.DeviceIdType.MESH
 rope_base = 1000000.0
 VMEM = pltpu.VMEM
-LAG = 1
+SUBS = 2
 AHEAD = 3
 BACK = 1
 
@@ -30,11 +30,11 @@
 
 
 def attend(
-    seq_count, tp_count, reach, chunk,
+    seq_count, tp_count, reach, chunk, team,
     tokens_hbm, gain_ref, wq_hbm, qb_ref, wk_hbm, kb_ref, wv_hbm, vb_ref, wo_hbm,
     kdoc_ref, near_hbm, far_ref, out_ref,
-    tokens, normed, wq, wkv, wo, near, q_ref, kv_ref, kv_in, kext, acc, tops, totals, sent, got,
-    load_sems, kv_send, kv_pass, kv_recv, send_sem, recv_sem,
+    tokens, normed, wq, wkv, wo, near, q_ref, kv_ref, kv_in, kext, acc, tops, totals, ctx, ctx_in, lent, sent, got,
+    load_sems, kv_send, kv_pass, kv_recv, send_sem, recv_sem, ctx_send, ctx_recv, lent_send, lent_recv,
 ):
     place = lax.axis_index("seq")
     turn = lax.axis_index("tp")
@@ -101,6 +101,51 @@
             for part in range(parts):
                 q_ref[part, HD:, :] = jnp.concatenate([veto[:, part * chunk:(part + 1) * chunk]] * heads, axis=1)
 
+    pl.semaphore_wait(barrier, near_count + sides)
+    half = tp_count // 2
+    right = turn // half
+    inner = (turn > 0) & (turn < tp_count - 1)
+    outer = jnp.logical_not(inner)
+    share = width // team
+    mine = lax.rem(place, team)
+    base = place - mine
+    partner = place + 1 - 2 * lax.rem(place, 2)
+    lent_cols = (tp_count - 1) * cols
+    steps = list(range(2, team, 2))
+
+    def lend():
+        rows_cut = pl.ds(pl.multiple_of(mine * share, 16), share)
+        cols_cut = pl.ds(pl.multiple_of((1 - right) * cols, HD), lent_cols)
+        return pltpu.make_async_remote_copy(
+            src_ref=wo_hbm.at[rows_cut, cols_cut], dst_ref=lent.at[rows_cut],
+            send_sem=lent_send.at[0], recv_sem=lent_recv.at[mine],
+            device_id={"tp": turn + 1 - 2 * right}, device_id_type=MESH,
+        )
+
+    def spread(piece_of, slot, target):
+        rows_cut = pl.ds(pl.multiple_of(piece_of * share, 16), share)
+        return pltpu.make_async_remote_copy(
+            src_ref=lent.at[rows_cut], dst_ref=lent.at[rows_cut],
+            send_sem=lent_send.at[slot], recv_sem=lent_recv.at[piece_of],
+            device_id={"seq": target}, device_id_type=MESH,
+        )
+
+    def own_spreads():
+        return [spread(mine, 1, partner)] + [
+            spread(mine, 2 + index, base + lax.rem(mine + away, team))
+            for index, away in enumerate(steps)
+        ]
+
+    def passed_spreads():
+        return [
+            spread(lax.rem(mine + team - away, team), 2 + len(steps) + index, partner)
+            for index, away in enumerate(steps)
+        ]
+
+    @pl.when(outer)
+    def _():
+        lend().start()
+
     gain = gain_ref[...].reshape(1, gain_ref.shape[0])
     for index in range(4):
         token_loads[index].wait()
@@ -133,10 +178,7 @@
     for lo in range(0, rows, HD):
         kv_ref[1, lo:lo + HD] = values[lo:lo + HD].T.astype(jnp.bfloat16)
 
-    pl.semaphore_wait(barrier, near_count + sides)
-
     odd = lax.rem(place, 2) == 1
-    partner = place + 1 - 2 * lax.rem(place, 2)
 
     def kv_copy(away):
         return pltpu.make_async_remote_copy(
@@ -207,49 +249,39 @@
         def _():
             relay(away, away - 1).start()
 
-    def term_copy(side, dest, part):
-        cut = pl.ds(pl.multiple_of(part * chunk, chunk), chunk)
-        target = lax.rem(turn + (1 if side == 0 else tp_count - 1), tp_count)
+    sub = chunk // SUBS
+
+    def sub_cut(index):
+        return pl.ds(pl.multiple_of(index * sub, sub), sub)
+
+    def term_copy(side, dest, index):
         return pltpu.make_async_remote_copy(
-            src_ref=sent.at[dest, cut], dst_ref=got.at[side, dest, cut],
-            send_sem=send_sem.at[dest, part], recv_sem=recv_sem.at[side, dest, part],
-            device_id={"tp": target}, device_id_type=MESH,
-        )
-
-    order = sorted(range(tp_count), key=lambda d: (-abs(2 * d - tp_count + 1), -d))
-
-    def forward(part, first):
-        cut = pl.ds(pl.multiple_of(part * chunk, chunk), chunk)
-        for side in (0, 1):
-            chosen = (2 * turn < tp_count) if (side == 0) == first else (2 * turn >= tp_count)
-            for dest in order:
-                inner = (turn > 0) & (dest > turn) if side == 0 else (
-                    (turn < tp_count - 1) & (dest < turn))
-
-                @pl.when(inner & chosen)
-                def _():
-                    term_copy(side, dest, part).wait_recv()
-                    sent[dest, cut] = (
-                        sent[dest, cut].astype(jnp.float32) + got[side, dest, cut].astype(jnp.float32)
-                    ).astype(jnp.bfloat16)
-                    term_copy(side, dest, part).start()
-
-    def finish(part):
-        cut = pl.ds(pl.multiple_of(part * chunk, chunk), chunk)
-        for dest in range(tp_count):
-            for side in (0, 1):
-                edge = (turn > 0) if side == 0 else (turn < tp_count - 1)
-
-                @pl.when((dest == turn) & edge)
-                def _():
-                    term_copy(side, dest, part).wait_recv()
-
-            @pl.when(dest == turn)
-            def _():
-                total = sent[dest, cut].astype(jnp.float32)
-                left = jnp.where(turn > 0, got[0, dest, cut].astype(jnp.float32), 0.0)
-                right = jnp.where(turn < tp_count - 1, got[1, dest, cut].astype(jnp.float32), 0.0)
-                out_ref[cut, :] = (total + left + right).astype(jnp.bfloat16)
+            src_ref=sent.at[dest, sub_cut(index)], dst_ref=got.at[side, dest, sub_cut(index)],
+            send_sem=send_sem.at[dest, index], recv_sem=recv_sem.at[side, dest, index],
+            device_id={"tp": turn + 1 - 2 * side}, device_id_type=MESH,
+        )
+
+    def ctx_copy(index):
+        return pltpu.make_async_remote_copy(
+            src_ref=ctx.at[sub_cut(index)], dst_ref=ctx_in.at[sub_cut(index)],
+            send_sem=ctx_send.at[index], recv_sem=ctx_recv.at[index],
+            device_id={"tp": turn + 1 - 2 * right}, device_id_type=MESH,
+        )
+
+    last = tp_count - 1
+    far = (1 - right) * last
+    home = right * last
+    across = last - turn
+    farther = (1 - right) * (last - 1) + right
+    beside = (1 - right) + right * (last - 1)
+
+    def forward(side, dest, index):
+        cut = sub_cut(index)
+        term_copy(side, dest, index).wait_recv()
+        sent[dest, cut] = (
+            sent[dest, cut].astype(jnp.float32) + got[side, dest, cut].astype(jnp.float32)
+        ).astype(jnp.bfloat16)
+        term_copy(side, dest, index).start()
 
     wide = step // chunk * chunk
     tiles = [(lo, min(wide, heads * chunk - lo)) for lo in range(0, heads * chunk, wide)]
@@ -307,6 +339,15 @@
                 gather(*mixed.pop(0))
 
         block(kv_ref, 0, True)
+        middle = (behind + 1) // 2
+
+        def between():
+            forward(right, across, 0)
+            forward(1 - right, home, 0)
+
+        @pl.when((part == 1) & inner & (middle == 0))
+        def _():
+            between()
 
         @pl.loop(1, behind + 1)
         def _(away):
@@ -314,54 +355,120 @@
             def _():
                 kv_copy(away).wait_recv()
 
+            @pl.when((part == 1) & inner & (away == middle))
+            def _():
+                between()
+
             block(kv_in.at[away - 1], away, False)
 
         whole = acc[...] * (1.0 / totals[...])
         context = jnp.concatenate(
             [whole[:, h * chunk:(h + 1) * chunk].T.astype(jnp.bfloat16) for h in range(heads)], axis=1
         )
+        ctx[cut, :] = context
+
+        @pl.when((part == 1) & outer)
+        def _():
+            for index in range(SUBS, 2 * SUBS):
+                ctx_copy(index).start()
+            for index in range(SUBS):
+                term_copy(right, beside, index).start()
 
         @pl.when(part == 0)
         def _():
             load.wait()
 
-        for dest in order:
+        for dest in range(tp_count):
             sent[dest, cut] = jnp.dot(
                 context, wo[:, dest * cols:(dest + 1) * cols], preferred_element_type=jnp.float32
             ).astype(jnp.bfloat16)
-        for dest in order:
-            @pl.when((turn == 0) & (dest > 0))
-            def _():
-                term_copy(0, dest, part).start()
-
-            @pl.when((turn == tp_count - 1) & (dest < tp_count - 1))
-            def _():
-                term_copy(1, dest, part).start()
-
-    @pl.loop(0, parts + LAG + 1)
+
+        @pl.when((part == 0) & outer)
+        def _():
+            for index in range(SUBS):
+                term_copy(right, across, index).start()
+                term_copy(right, farther, index).start()
+
+        @pl.when((part == 0) & inner)
+        def _():
+            spread(mine, 1, partner).wait_recv()
+            for copy in own_spreads():
+                copy.start()
+            forward(right, far, 0)
+
+    @pl.loop(0, 2)
     def _(part):
-        @pl.when(part < parts)
-        def _():
-            piece(part)
-
-        @pl.when((part >= LAG) & (part < parts + LAG))
-        def _():
-            forward(part - LAG, True)
-
-        @pl.when(part >= LAG + 1)
-        def _():
-            forward(part - LAG - 1, False)
-
-    @pl.loop(0, parts)
-    def _(part):
-        finish(part)
-
-    @pl.loop(0, parts)
-    def _(part):
-        for dest in range(tp_count):
-            @pl.when(dest != turn)
-            def _():
-                term_copy(0, dest, part).wait_send()
+        piece(part)
+
+    @pl.when(inner)
+    def _():
+        for index in range(1, SUBS):
+            forward(right, far, index)
+            forward(right, across, index)
+            forward(1 - right, home, index)
+        for copy in passed_spreads():
+            copy.wait_recv()
+            copy.start()
+        other = mine + 1 - 2 * lax.rem(mine, 2)
+        for away in [0] + steps:
+            spread(lax.rem(other + away, team), 1, partner).wait_recv()
+
+        @pl.loop(SUBS, 2 * SUBS)
+        def _(index):
+            cut = sub_cut(index)
+            ctx_copy(index).wait_recv()
+            guest = ctx_in[cut, :]
+            for at in range(tp_count - 1):
+                dest = at + 1 - right
+                sent[dest, cut] = (
+                    sent[dest, cut].astype(jnp.float32)
+                    + jnp.dot(
+                        guest, lent[:, at * cols:(at + 1) * cols], preferred_element_type=jnp.float32
+                    )
+                ).astype(jnp.bfloat16)
+            term_copy(right, far, index).start()
+            term_copy(right, across, index).start()
+
+        for index in range(SUBS, 2 * SUBS):
+            forward(1 - right, home, index)
+
+    @pl.loop(0, 2 * SUBS)
+    def _(index):
+        cut = sub_cut(index)
+        term_copy(1 - right, turn, index).wait_recv()
+        total = sent[turn, cut].astype(jnp.float32) + got[1 - right, turn, cut].astype(jnp.float32)
+        both = inner & (index < SUBS)
+
+        @pl.when(both)
+        def _():
+            term_copy(right, turn, index).wait_recv()
+            out_ref[cut, :] = (total + got[right, turn, cut].astype(jnp.float32)).astype(jnp.bfloat16)
+
+        @pl.when(jnp.logical_not(both))
+        def _():
+            out_ref[cut, :] = total.astype(jnp.bfloat16)
+
+    @pl.loop(0, 2 * SUBS)
+    def _(index):
+        @pl.when(inner | (index < SUBS))
+        def _():
+            for dest in range(tp_count):
+                @pl.when(dest != turn)
+                def _():
+                    term_copy(right, dest, index).wait_send()
+
+        @pl.when(outer & (index >= SUBS))
+        def _():
+            ctx_copy(index).wait_send()
+
+    @pl.when(outer)
+    def _():
+        lend().wait_send()
+
+    @pl.when(inner)
+    def _():
+        for copy in own_spreads() + passed_spreads():
+            copy.wait_send()
 
     each_send(lambda copy: copy.wait_send())
     each_relay(lambda copy: copy.wait_send())
@@ -377,6 +484,8 @@
     cols = o_weight.shape[1] // tp_count
     reach = min(seq_count - 1, (seq_count * rows // 2 + 2 * rows - 2) // rows)
     chunk = rows // 2
+    team = math.gcd(seq_count, 8)
+    subs = rows // chunk * SUBS
     parts = rows // chunk
     near, far = rope_tables(rows, seq_count)
     hbm = pl.BlockSpec(memory_space=pl.ANY)
@@ -385,7 +494,7 @@
     spans = -(-width // (2 * HD))
     kdoc = doc_ids.reshape(seq_count, 1, rows)
     return pl.pallas_call(
-        functools.partial(attend, seq_count, tp_count, reach, chunk),
+        functools.partial(attend, seq_count, tp_count, reach, chunk, team),
         out_shape=jax.ShapeDtypeStruct((rows, cols), jnp.bfloat16),
         in_specs=[hbm, vmem, hbm, vmem, hbm, vmem, hbm, vmem, hbm, vmem, hbm, vmem],
         out_specs=vmem,
@@ -403,14 +512,21 @@
             VMEM((HD, width // HD * chunk), jnp.float32),
             VMEM((1, width // HD * chunk), jnp.float32),
             VMEM((1, width // HD * chunk), jnp.float32),
+            VMEM((rows, width), jnp.bfloat16),
+            VMEM((rows, width), jnp.bfloat16),
+            VMEM((width, (tp_count - 1) * cols), jnp.bfloat16),
             VMEM((tp_count, rows, cols), jnp.bfloat16),
             VMEM((2, tp_count, rows, cols), jnp.bfloat16),
             pltpu.SemaphoreType.DMA((8 + spans,)),
             pltpu.SemaphoreType.DMA((slots,)),
             pltpu.SemaphoreType.DMA((slots,)),
             pltpu.SemaphoreType.DMA((slots,)),
-            pltpu.SemaphoreType.DMA((tp_count, parts)),
-            pltpu.SemaphoreType.DMA((2, tp_count, parts)),
+            pltpu.SemaphoreType.DMA((tp_count, subs)),
+            pltpu.SemaphoreType.DMA((2, tp_count, subs)),
+            pltpu.SemaphoreType.DMA((subs,)),
+            pltpu.SemaphoreType.DMA((subs,)),
+            pltpu.SemaphoreType.DMA((2 * team,)),
+            pltpu.SemaphoreType.DMA((team,)),
         ],
         compiler_params=pltpu.CompilerParams(
             collective_id=0, has_side_effects=True, vmem_limit_bytes=56 * 1024 * 1024

time: 113 us -> 89.2 us (0.79)
  the two profiles are of different devices: /device:TPU:28 before, /device:TPU:4 now
where the time goes in v2:
time: 89.2 us; the launch traced here: 88.9 us
  Pallas kernels  86.8 us (97%)
  local copies, waits for them, and re-layouts  2.18 us (2%)
    pallas_call x1, Pallas kernels, body(): pl.pallas_call(functools.partial(attend, seq_count, tp_count, reach, chun...  86.8 us
    unnamed x1, local copies, waits for them, and re-layouts  2.18 us

profile of v2, /device:TPU:4, one launch (start us, length us, event | category | flops | bytes accessed | tf_op | source)
XLA Modules:
  0.0 88.9 jit_solution(4855756834715636064)
XLA Ops:
  0.0 86.8 %shard_map.118 = bf16[512,896]{1,0:T(8,128)(2,1)} custom-call(bf16[512,3584]{1,0:T(8,128)(2,1)} %tokens_hbm.1, f32[3584]{0:T(1024)} %gain_ref.1, bf16[3584,896]{1,0:T(8,128)(2,1)} %wq_hbm.1, f32[896]{0:T(1024)} %qb_ref.1, bf16[3584,128]{1,0:T(8,128)(2,1)} %wk_hbm.1, f32[128]{0:T(128)} %kb_ref.1, bf16[3584,128]{1,0:T(8,128)(2,1)} %wv_hbm.1, f32[128]{0:T(128)} %vb_ref.1, ...), custom_call_target="tpu_custom_call" | custom-call | tf_op jit(solution)/shard_map/pallas_call | solution.py:496
  86.8 2.2 %copy.14 = bf16[512,896]{1,0:T(8,128)(2,1)} copy(bf16[512,896]{1,0:T(8,128)(2,1)} %shard_map.118) | data formatting | bytes 1835008

commit v3 on v2

--- a/solution.py
+++ b/solution.py
@@ -34,7 +34,7 @@
     tokens_hbm, gain_ref, wq_hbm, qb_ref, wk_hbm, kb_ref, wv_hbm, vb_ref, wo_hbm,
     kdoc_ref, near_hbm, far_ref, out_ref,
     tokens, normed, wq, wkv, wo, near, q_ref, kv_ref, kv_in, kext, acc, tops, totals, ctx, ctx_in, lent, sent, got,
-    load_sems, kv_send, kv_pass, kv_recv, send_sem, recv_sem, ctx_send, ctx_recv, lent_send, lent_recv,
+    load_sems, kv_send, kv_pass, kv_recv, kv_back, send_sem, recv_sem, ctx_send, ctx_recv, lent_send, lent_recv,
 ):
     place = lax.axis_index("seq")
     turn = lax.axis_index("tp")
@@ -180,52 +180,114 @@
 
     odd = lax.rem(place, 2) == 1
 
-    def kv_copy(away):
+    core = lax.rem(place, 2)
+    bent = lax.rem(place // 2, 2) == 1
+    bends = reach >= 4
+
+    def kv_copy(away, part):
         return pltpu.make_async_remote_copy(
-            src_ref=kv_ref, dst_ref=kv_in.at[away - 1],
-            send_sem=kv_send.at[away - 1], recv_sem=kv_recv.at[away - 1],
+            src_ref=kv_ref.at[part], dst_ref=kv_in.at[away - 1, part],
+            send_sem=kv_send.at[away - 1, part], recv_sem=kv_recv.at[away - 1, part],
             device_id={"seq": lax.rem(place + away, seq_count)}, device_id_type=MESH,
         )
 
-    def relay(away, landing):
+    def relay(away, landing, part):
         return pltpu.make_async_remote_copy(
-            src_ref=kv_in.at[away - 1], dst_ref=kv_in.at[landing - 1],
-            send_sem=kv_pass.at[away - 1], recv_sem=kv_recv.at[landing - 1],
+            src_ref=kv_in.at[away - 1, part], dst_ref=kv_in.at[landing - 1, part],
+            send_sem=kv_pass.at[away - 1, part], recv_sem=kv_recv.at[landing - 1, part],
             device_id={"seq": partner}, device_id_type=MESH,
         )
 
+    def back(part):
+        return pltpu.make_async_remote_copy(
+            src_ref=kv_in.at[3, part], dst_ref=kv_in.at[1, part],
+            send_sem=kv_back.at[part], recv_sem=kv_recv.at[1, part],
+            device_id={"seq": lax.rem(place + seq_count - 2, seq_count)}, device_id_type=MESH,
+        )
+
     evens = [away for away in range(2, reach + 2, 2) if away < seq_count]
+    backs = bent & (place >= 4) & bends
 
     def wanted(away):
         return odd if away > reach else (place >= 0)
 
     def each_send(act):
-        for away in evens:
-            @pl.when((place + away < seq_count) & wanted(away))
+        for part in (0, 1):
+            for away in evens:
+                direct = jnp.logical_not(bent & (place + 4 < seq_count) & bends & (away == 2))
+
+                @pl.when((place + away < seq_count) & wanted(away) & direct)
+                def _():
+                    act(kv_copy(away, part))
+
+            @pl.when(jnp.logical_not(odd))
             def _():
-                act(kv_copy(away))
-
-        @pl.when(jnp.logical_not(odd))
-        def _():
-            act(kv_copy(1))
+                act(kv_copy(1, part))
 
     def each_relay(act):
-        for away in evens:
-            if away + 1 <= reach:
-                @pl.when((place >= away) & jnp.logical_not(odd))
+        for part in (0, 1):
+            for away in evens:
+                if away + 1 <= reach:
+                    @pl.when((place >= away) & jnp.logical_not(odd))
+                    def _():
+                        act(relay(away, away + 1, part))
+
+                @pl.when((place >= away) & odd)
                 def _():
-                    act(relay(away, away + 1))
-
-            @pl.when((place >= away) & odd)
+                    act(relay(away, away - 1, part))
+
+            if bends:
+                @pl.when(backs)
+                def _():
+                    act(back(part))
+
+    def take(group):
+        for part in (0, 1):
+            @pl.when(jnp.logical_not(backs & (group == 4)))
             def _():
-                act(relay(away, away - 1))
+                kv_copy(group, part).wait_recv()
+
+            @pl.when(odd | (group + 1 <= reach))
+            def _():
+                relay(group, group + 1 - 2 * core, part).start()
+
+    def obtain(away):
+        even = lax.rem(away, 2) == 0
+
+        @pl.when(even & (jnp.logical_not(odd) | (away == behind)))
+        def _():
+            take(away)
+
+        @pl.when(jnp.logical_not(even) & odd & (away > 2))
+        def _():
+            take(away - 1)
+
+        if evens and evens[-1] > reach:
+            @pl.when((away == 1) & odd & (place >= evens[-1]))
+            def _():
+                take(evens[-1])
+
+        @pl.when(jnp.logical_not(even))
+        def _():
+            for part in (0, 1):
+                kv_copy(away, part).wait_recv()
+
+    def bounce(part):
+        if bends:
+            @pl.when(backs)
+            def _():
+                kv_copy(4, part).wait_recv()
+                back(part).start()
 
     each_send(lambda copy: copy.start())
 
-    for index, (lo, size) in enumerate(spans):
-        q_loads[index].wait()
-        if index == 1:
+    for index in range(0, len(spans), 2):
+        for copy in q_loads[index:index + 2]:
+            copy.wait()
+        if index == 0:
             load.start()
+        lo = spans[index][0]
+        size = sum(extent for _, extent in spans[index:index + 2])
         out = jnp.dot(
             normed[...], wq[:, lo:lo + size], preferred_element_type=jnp.float32
         ) + qb_ref[lo:lo + size].reshape(1, size)
@@ -235,19 +297,10 @@
             for part in range(parts):
                 q_ref[part, :HD, at:at + chunk] = turned[part * chunk:(part + 1) * chunk].T.astype(jnp.bfloat16)
 
-    for away in evens:
-        @pl.when((place >= away) & wanted(away))
-        def _():
-            kv_copy(away).wait_recv()
-
-        if away + 1 <= reach:
-            @pl.when((place >= away) & jnp.logical_not(odd))
-            def _():
-                relay(away, away + 1).start()
-
-        @pl.when((place >= away) & odd)
-        def _():
-            relay(away, away - 1).start()
+    def offer():
+        spread(mine, 1, partner).wait_recv()
+        for copy in own_spreads():
+            copy.start()
 
     sub = chunk // SUBS
 
@@ -338,28 +391,44 @@
             while mixed:
                 gather(*mixed.pop(0))
 
+        @pl.when(part == 0)
+        def _():
+            bounce(0)
+
         block(kv_ref, 0, True)
         middle = (behind + 1) // 2
 
         def between():
-            forward(right, across, 0)
+            forward(right, far, 1)
             forward(1 - right, home, 0)
 
+        @pl.when(part == 0)
+        def _():
+            bounce(1)
+
         @pl.when((part == 1) & inner & (middle == 0))
         def _():
             between()
 
+        tail = (1 - core) * (behind // reach) * (reach % 2) if reach else 0
+
         @pl.loop(1, behind + 1)
-        def _(away):
-            @pl.when((part == 0) & (lax.rem(away, 2) == 1))
+        def _(turned):
+            away = lax.rem(2 * behind - turned - tail, behind) + 1
+
+            @pl.when(part == 0)
             def _():
-                kv_copy(away).wait_recv()
-
-            @pl.when((part == 1) & inner & (away == middle))
+                obtain(away)
+
+            @pl.when((part == 1) & inner & (turned == middle))
             def _():
                 between()
 
             block(kv_in.at[away - 1], away, False)
+
+        @pl.when((part == 0) & inner & (behind > 1))
+        def _():
+            offer()
 
         whole = acc[...] * (1.0 / totals[...])
         context = jnp.concatenate(
@@ -385,15 +454,16 @@
 
         @pl.when((part == 0) & outer)
         def _():
-            for index in range(SUBS):
-                term_copy(right, across, index).start()
-                term_copy(right, farther, index).start()
+            for dest in (across, farther):
+                for index in range(SUBS):
+                    term_copy(right, dest, index).start()
+
+        @pl.when((part == 0) & inner & (behind < 2))
+        def _():
+            offer()
 
         @pl.when((part == 0) & inner)
         def _():
-            spread(mine, 1, partner).wait_recv()
-            for copy in own_spreads():
-                copy.start()
             forward(right, far, 0)
 
     @pl.loop(0, 2)
@@ -402,9 +472,11 @@
 
     @pl.when(inner)
     def _():
+        for index in range(2, SUBS):
+            forward(right, far, index)
+        for index in range(SUBS):
+            forward(right, across, index)
         for index in range(1, SUBS):
-            forward(right, far, index)
-            forward(right, across, index)
             forward(1 - right, home, index)
         for copy in passed_spreads():
             copy.wait_recv()
@@ -427,8 +499,9 @@
                     )
                 ).astype(jnp.bfloat16)
             term_copy(right, far, index).start()
+
+        for index in range(SUBS, 2 * SUBS):
             term_copy(right, across, index).start()
-
         for index in range(SUBS, 2 * SUBS):
             forward(1 - right, home, index)
 
@@ -518,9 +591,10 @@
             VMEM((tp_count, rows, cols), jnp.bfloat16),
             VMEM((2, tp_count, rows, cols), jnp.bfloat16),
             pltpu.SemaphoreType.DMA((8 + spans,)),
-            pltpu.SemaphoreType.DMA((slots,)),
-            pltpu.SemaphoreType.DMA((slots,)),
-            pltpu.SemaphoreType.DMA((slots,)),
+            pltpu.SemaphoreType.DMA((slots, 2)),
+            pltpu.SemaphoreType.DMA((slots, 2)),
+            pltpu.SemaphoreType.DMA((slots, 2)),
+            pltpu.SemaphoreType.DMA((2,)),
             pltpu.SemaphoreType.DMA((tp_count, subs)),
             pltpu.SemaphoreType.DMA((2, tp_count, subs)),
             pltpu.SemaphoreType.DMA((subs,)),

time: 89.2 us -> 80.5 us (0.902)
  the two profiles are of different devices: /device:TPU:4 before, /device:TPU:13 now
where the time goes in v3:
time: 80.5 us; the launch traced here: 80.2 us
  Pallas kernels  78.1 us (97%)
  local copies, waits for them, and re-layouts  2.18 us (3%)
    pallas_call x1, Pallas kernels, body(): pl.pallas_call(functools.partial(attend, seq_count, tp_count, reach, chun...  78.1 us
    unnamed x1, local copies, waits for them, and re-layouts  2.18 us

profile of v3, /device:TPU:13, one launch (start us, length us, event | category | flops | bytes accessed | tf_op | source)
XLA Modules:
  0.0 80.2 jit_solution(15970896511741018213)
XLA Ops:
  0.0 78.1 %shard_map.118 = bf16[512,896]{1,0:T(8,128)(2,1)} custom-call(bf16[512,3584]{1,0:T(8,128)(2,1)} %tokens_hbm.1, f32[3584]{0:T(1024)} %gain_ref.1, bf16[3584,896]{1,0:T(8,128)(2,1)} %wq_hbm.1, f32[896]{0:T(1024)} %qb_ref.1, bf16[3584,128]{1,0:T(8,128)(2,1)} %wk_hbm.1, f32[128]{0:T(128)} %kb_ref.1, bf16[3584,128]{1,0:T(8,128)(2,1)} %wv_hbm.1, f32[128]{0:T(128)} %vb_ref.1, ...), custom_call_target="tpu_custom_call" | custom-call | tf_op jit(solution)/shard_map/pallas_call | solution.py:569
  78.1 2.2 %copy.14 = bf16[512,896]{1,0:T(8,128)(2,1)} copy(bf16[512,896]{1,0:T(8,128)(2,1)} %shard_map.118) | data formatting | bytes 1835008

commit v4 on v3

--- a/solution.py
+++ b/solution.py
@@ -13,7 +13,8 @@
 MESH = pl.DeviceIdType.MESH
 rope_base = 1000000.0
 VMEM = pltpu.VMEM
-SUBS = 2
+SUBS = 4
+TERMS = 5
 AHEAD = 3
 BACK = 1
 
@@ -31,9 +32,9 @@
 
 def attend(
     seq_count, tp_count, reach, chunk, team,
-    tokens_hbm, gain_ref, wq_hbm, qb_ref, wk_hbm, kb_ref, wv_hbm, vb_ref, wo_hbm,
-    kdoc_ref, near_hbm, far_ref, out_ref,
-    tokens, normed, wq, wkv, wo, near, q_ref, kv_ref, kv_in, kext, acc, tops, totals, ctx, ctx_in, lent, sent, got,
+    tokens_hbm, gain_hbm, wq_hbm, qb_hbm, wk_hbm, kb_hbm, wv_hbm, vb_hbm, wo_hbm,
+    kdoc_hbm, near_hbm, far_hbm, out_ref,
+    gain_ref, qb_ref, kb_ref, vb_ref, kdoc_ref, far_ref, tokens, normed, wq, wkv, wo, near, q_ref, kv_ref, kv_in, kext, acc, tops, totals, ctx, ctx_in, lent, sent, got,
     load_sems, kv_send, kv_pass, kv_recv, kv_back, send_sem, recv_sem, ctx_send, ctx_recv, lent_send, lent_recv,
 ):
     place = lax.axis_index("seq")
@@ -65,7 +66,14 @@
         for index, (lo, size) in enumerate(spans)
     ]
     load = pltpu.make_async_copy(wo_hbm, wo, load_sems.at[7 + len(spans)])
-    for copy in token_loads + kv_loads + [near_load]:
+    small = [
+        pltpu.make_async_copy(source, target, load_sems.at[8 + len(spans) + index])
+        for index, (source, target) in enumerate([
+            (kdoc_hbm, kdoc_ref), (gain_hbm, gain_ref), (far_hbm, far_ref),
+            (kb_hbm, kb_ref), (vb_hbm, vb_ref), (qb_hbm, qb_ref),
+        ])
+    ]
+    for copy in small + token_loads + kv_loads + [near_load]:
         copy.start()
 
     barrier = pltpu.get_barrier_semaphore()
@@ -91,6 +99,7 @@
     near_count = jnp.minimum(place, span) + jnp.minimum(seq_count - 1 - place, span)
     sides = jnp.where(turn > 0, 1, 0) + jnp.where(turn < tp_count - 1, 1, 0)
 
+    small[0].wait()
     lane = lax.broadcasted_iota(jnp.int32, (rows, HD), 1)
     doc = lax.broadcasted_iota(jnp.int32, (HD, rows), 0)
     for away in range(reach + 1):
@@ -130,22 +139,50 @@
             device_id={"seq": target}, device_id_type=MESH,
         )
 
+    def mirror(index, bits):
+        moved = index
+        bit = 1
+        while bit < team:
+            if bits // bit % 2:
+                moved = moved + bit - 2 * bit * lax.rem(index // bit, 2)
+            bit *= 2
+        return moved
+
+    straight = [bits for bits in steps if bits & (bits - 1) == 0]
+
     def own_spreads():
         return [spread(mine, 1, partner)] + [
-            spread(mine, 2 + index, base + lax.rem(mine + away, team))
-            for index, away in enumerate(steps)
+            spread(mine, 2 + index, base + mirror(mine, bits)) for index, bits in enumerate(straight)
         ]
 
-    def passed_spreads():
-        return [
-            spread(lax.rem(mine + team - away, team), 2 + len(steps) + index, partner)
-            for index, away in enumerate(steps)
-        ]
+    def passed_spread(index):
+        return spread(mirror(mine, steps[index]), 2 + len(steps) + index, partner)
+
+    def cross():
+        a, b = mirror(mine, straight[0]), mirror(mine, straight[-1])
+        side = lax.rem(mine, 2)
+        return spread((1 - side) * a + side * b, 1 + len(steps), base + (1 - side) * b + side * a)
+
+    def hand_over(wanted_steps):
+        for index, bits in enumerate(steps):
+            if bits in wanted_steps:
+                copy = passed_spread(index)
+                copy.wait_recv()
+                copy.start()
+
+    bent_steps = [bits for bits in steps if bits not in straight]
+
+    def pass_straight():
+        hand_over(straight)
+        if bent_steps:
+            cross().start()
 
     @pl.when(outer)
     def _():
         lend().start()
 
+    for copy in small[1:]:
+        copy.wait()
     gain = gain_ref[...].reshape(1, gain_ref.shape[0])
     for index in range(4):
         token_loads[index].wait()
@@ -263,7 +300,7 @@
             take(away - 1)
 
         if evens and evens[-1] > reach:
-            @pl.when((away == 1) & odd & (place >= evens[-1]))
+            @pl.when((away == 2) & odd & (place >= evens[-1]))
             def _():
                 take(evens[-1])
 
@@ -324,9 +361,8 @@
     last = tp_count - 1
     far = (1 - right) * last
     home = right * last
-    across = last - turn
     farther = (1 - right) * (last - 1) + right
-    beside = (1 - right) + right * (last - 1)
+    other = turn + 1 - 2 * lax.rem(turn, 2)
 
     def forward(side, dest, index):
         cut = sub_cut(index)
@@ -335,6 +371,15 @@
             sent[dest, cut].astype(jnp.float32) + got[side, dest, cut].astype(jnp.float32)
         ).astype(jnp.bfloat16)
         term_copy(side, dest, index).start()
+
+    def event(index):
+        @pl.when(index < 2 * SUBS)
+        def _():
+            forward(right, far + index // SUBS * (farther - far), lax.rem(index, SUBS))
+
+        @pl.when((index > 1) & (index < SUBS + 2))
+        def _():
+            forward(1 - right, home, index - 2)
 
     wide = step // chunk * chunk
     tiles = [(lo, min(wide, heads * chunk - lo)) for lo in range(0, heads * chunk, wide)]
@@ -396,39 +441,33 @@
             bounce(0)
 
         block(kv_ref, 0, True)
-        middle = (behind + 1) // 2
-
-        def between():
-            forward(right, far, 1)
-            forward(1 - right, home, 0)
-
         @pl.when(part == 0)
         def _():
             bounce(1)
-
-        @pl.when((part == 1) & inner & (middle == 0))
-        def _():
-            between()
 
         tail = (1 - core) * (behind // reach) * (reach % 2) if reach else 0
 
         @pl.loop(1, behind + 1)
         def _(turned):
-            away = lax.rem(2 * behind - turned - tail, behind) + 1
+            away = lax.rem(2 * behind - turned - tail + core, behind) + 1
 
             @pl.when(part == 0)
             def _():
                 obtain(away)
 
-            @pl.when((part == 1) & inner & (turned == middle))
-            def _():
-                between()
+            @pl.when((part == 0) & inner & (behind > 1) & (turned == behind))
+            def _():
+                offer()
+
+            @pl.when((part == 1) & inner)
+            def _():
+                event(turned - 1)
+
+            @pl.when((part == 1) & inner & (turned == behind - 1) & (behind > 4))
+            def _():
+                pass_straight()
 
             block(kv_in.at[away - 1], away, False)
-
-        @pl.when((part == 0) & inner & (behind > 1))
-        def _():
-            offer()
 
         whole = acc[...] * (1.0 / totals[...])
         context = jnp.concatenate(
@@ -436,35 +475,58 @@
         )
         ctx[cut, :] = context
 
+        @pl.when((part == 1) & inner)
+        def _():
+            event(behind)
+
+            @pl.when((behind > 1) & (behind < 5))
+            def _():
+                pass_straight()
+
+        @pl.when(part == 0)
+        def _():
+            load.wait()
+
+        def term(dest):
+            sent[dest, cut] = jnp.dot(
+                context, wo[:, pl.ds(pl.multiple_of(dest * cols, HD), cols)],
+                preferred_element_type=jnp.float32,
+            ).astype(jnp.bfloat16)
+
+        def launch(dest):
+            @pl.when((part == 0) & outer)
+            def _():
+                for index in range(SUBS):
+                    term_copy(right, dest, index).start()
+
+            @pl.when((part == 1) & outer)
+            def _():
+                for index in range(SUBS, TERMS):
+                    term_copy(right, dest, index).start()
+
+        term(far)
+        launch(far)
+        term(farther)
+        launch(farther)
+
         @pl.when((part == 1) & outer)
         def _():
-            for index in range(SUBS, 2 * SUBS):
+            for index in range(TERMS, 2 * SUBS):
                 ctx_copy(index).start()
             for index in range(SUBS):
-                term_copy(right, beside, index).start()
-
-        @pl.when(part == 0)
-        def _():
-            load.wait()
-
-        for dest in range(tp_count):
-            sent[dest, cut] = jnp.dot(
-                context, wo[:, dest * cols:(dest + 1) * cols], preferred_element_type=jnp.float32
-            ).astype(jnp.bfloat16)
-
-        @pl.when((part == 0) & outer)
-        def _():
-            for dest in (across, farther):
-                for index in range(SUBS):
-                    term_copy(right, dest, index).start()
+                term_copy(right, other, index).start()
+
+        term(other)
+        term(turn)
+
+        @pl.when((part == 1) & outer)
+        def _():
+            for index in range(SUBS, TERMS):
+                term_copy(right, other, index).start()
 
         @pl.when((part == 0) & inner & (behind < 2))
         def _():
             offer()
-
-        @pl.when((part == 0) & inner)
-        def _():
-            forward(right, far, 0)
 
     @pl.loop(0, 2)
     def _(part):
@@ -472,20 +534,38 @@
 
     @pl.when(inner)
     def _():
-        for index in range(2, SUBS):
+        split = jnp.where(behind > 1, behind + 1, 2 * SUBS - 1)
+        early = (behind > 4) & (behind < 2 * SUBS - 2)
+
+        @pl.loop(behind + 1, split)
+        def _(index):
+            event(index)
+
+        @pl.when(behind < 2)
+        def _():
+            pass_straight()
+
+        @pl.loop(split, 2 * SUBS)
+        def _(index):
+            event(index)
+
+            @pl.when((index == 2 * SUBS - 2) & early)
+            def _():
+                hand_over(bent_steps)
+
+        for index in range(SUBS, TERMS):
             forward(right, far, index)
-        for index in range(SUBS):
-            forward(right, across, index)
-        for index in range(1, SUBS):
-            forward(1 - right, home, index)
-        for copy in passed_spreads():
-            copy.wait_recv()
-            copy.start()
-        other = mine + 1 - 2 * lax.rem(mine, 2)
-        for away in [0] + steps:
-            spread(lax.rem(other + away, team), 1, partner).wait_recv()
-
-        @pl.loop(SUBS, 2 * SUBS)
+            forward(right, farther, index)
+
+        @pl.when(jnp.logical_not(early))
+        def _():
+            hand_over(bent_steps)
+
+        twin = mine + 1 - 2 * lax.rem(mine, 2)
+        for bits in [0] + steps:
+            spread(mirror(twin, bits), 1, partner).wait_recv()
+
+        @pl.loop(TERMS, 2 * SUBS)
         def _(index):
             cut = sub_cut(index)
             ctx_copy(index).wait_recv()
@@ -500,8 +580,8 @@
                 ).astype(jnp.bfloat16)
             term_copy(right, far, index).start()
 
-        for index in range(SUBS, 2 * SUBS):
-            term_copy(right, across, index).start()
+        for index in range(TERMS, 2 * SUBS):
+            term_copy(right, farther, index).start()
         for index in range(SUBS, 2 * SUBS):
             forward(1 - right, home, index)
 
@@ -510,7 +590,7 @@
         cut = sub_cut(index)
         term_copy(1 - right, turn, index).wait_recv()
         total = sent[turn, cut].astype(jnp.float32) + got[1 - right, turn, cut].astype(jnp.float32)
-        both = inner & (index < SUBS)
+        both = inner & (index < TERMS)
 
         @pl.when(both)
         def _():
@@ -523,14 +603,14 @@
 
     @pl.loop(0, 2 * SUBS)
     def _(index):
-        @pl.when(inner | (index < SUBS))
+        @pl.when(inner | (index < TERMS))
         def _():
             for dest in range(tp_count):
                 @pl.when(dest != turn)
                 def _():
                     term_copy(right, dest, index).wait_send()
 
-        @pl.when(outer & (index >= SUBS))
+        @pl.when(outer & (index >= TERMS))
         def _():
             ctx_copy(index).wait_send()
 
@@ -540,8 +620,10 @@
 
     @pl.when(inner)
     def _():
-        for copy in own_spreads() + passed_spreads():
+        for copy in own_spreads() + [passed_spread(index) for index in range(len(steps))]:
             copy.wait_send()
+        if len(straight) < len(steps):
+            cross().wait_send()
 
     each_send(lambda copy: copy.wait_send())
     each_relay(lambda copy: copy.wait_send())
@@ -561,7 +643,7 @@
     subs = rows // chunk * SUBS
     parts = rows // chunk
     near, far = rope_tables(rows, seq_count)
-    hbm = pl.BlockSpec(memory_space=pl.ANY)
+    hbm = pl.BlockSpec(memory_space=pltpu.HBM)
     vmem = pl.BlockSpec(memory_space=VMEM)
     slots = reach + 1
     spans = -(-width // (2 * HD))
@@ -569,9 +651,15 @@
     return pl.pallas_call(
         functools.partial(attend, seq_count, tp_count, reach, chunk, team),
         out_shape=jax.ShapeDtypeStruct((rows, cols), jnp.bfloat16),
-        in_specs=[hbm, vmem, hbm, vmem, hbm, vmem, hbm, vmem, hbm, vmem, hbm, vmem],
+        in_specs=[hbm] * 12,
         out_specs=vmem,
         scratch_shapes=[
+            VMEM(norm_gain.shape, jnp.float32),
+            VMEM(q_bias.shape, jnp.float32),
+            VMEM(k_bias.shape, jnp.float32),
+            VMEM(v_bias.shape, jnp.float32),
+            VMEM(kdoc.shape, jnp.int32),
+            VMEM(far.shape, jnp.float32),
             VMEM((rows, model), jnp.bfloat16),
             VMEM((rows, model), jnp.bfloat16),
             VMEM((model, width), jnp.bfloat16),
@@ -590,7 +678,7 @@
             VMEM((width, (tp_count - 1) * cols), jnp.bfloat16),
             VMEM((tp_count, rows, cols), jnp.bfloat16),
             VMEM((2, tp_count, rows, cols), jnp.bfloat16),
-            pltpu.SemaphoreType.DMA((8 + spans,)),
+            pltpu.SemaphoreType.DMA((14 + spans,)),
             pltpu.SemaphoreType.DMA((slots, 2)),
             pltpu.SemaphoreType.DMA((slots, 2)),
             pltpu.SemaphoreType.DMA((slots, 2)),
@@ -603,11 +691,16 @@
             pltpu.SemaphoreType.DMA((team,)),
         ],
         compiler_params=pltpu.CompilerParams(
-            collective_id=0, has_side_effects=True, vmem_limit_bytes=56 * 1024 * 1024
+            collective_id=0, has_side_effects=True, vmem_limit_bytes=52 * 1024 * 1024
         ),
     )(
-        tokens, norm_gain, q_weight, q_bias, k_weight, k_bias, v_weight, v_bias, o_weight,
-        kdoc, jnp.asarray(near), jnp.asarray(far),
+        *[
+            pltpu.with_memory_space_constraint(item, pltpu.HBM)
+            for item in (
+                tokens, norm_gain, q_weight, q_bias, k_weight, k_bias, v_weight, v_bias, o_weight,
+                kdoc, jnp.asarray(near), jnp.asarray(far),
+            )
+        ]
     )
 
 

time: 80.5 us -> 72.8 us (0.904)
  Pallas kernels: 78.1 us -> 71.6 us
  local copies, waits for them, and re-layouts: 2.18 us -> 0.93 us
    pallas_call x1, Pallas kernels: 78.1 us -> 71.6 us  [body(): pl.pallas_call(functools.partial(attend, seq_count, tp_count, reach, chun...]
    unnamed x1, local copies, waits for them, and re-layouts: 2.18 us -> 0.93 us
where the time goes in v4:
time: 72.8 us; the launch traced here: 72.6 us
  Pallas kernels  71.6 us (98%)
  local copies, waits for them, and re-layouts  0.93 us (1%)
    pallas_call x1, Pallas kernels, body(): pl.pallas_call(functools.partial(attend, seq_count, tp_count, reach, chun...  71.6 us

profile of v4, /device:TPU:13, one launch (start us, length us, event | category | flops | bytes accessed | tf_op | source)
XLA Modules:
  0.0 72.6 jit_solution(16974730161224700161)
XLA Ops:
  0.0 71.6 %shard_map.118 = bf16[512,896]{1,0:T(8,128)(2,1)S(1)} custom-call(bf16[512,3584]{1,0:T(8,128)(2,1)} %tokens_hbm.1, f32[3584]{0:T(1024)} %gain_hbm.1, bf16[3584,896]{1,0:T(8,128)(2,1)} %wq_hbm.1, f32[896]{0:T(1024)} %qb_hbm.1, bf16[3584,128]{1,0:T(8,128)(2,1)} %wk_hbm.1, f32[128]{0:T(128)} %kb_hbm.1, bf16[3584,128]{1,0:T(8,128)(2,1)} %wv_hbm.1, f32[128]{0:T(128)} %vb_hbm.1, ...), custom_call_target="tpu_custom_call" | custom-call | tf_op jit(solution)/shard_map/pallas_call | solution.py:651
  71.6 0.9 %copy.14 = bf16[512,896]{1,0:T(8,128)(2,1)} copy(bf16[512,896]{1,0:T(8,128)(2,1)S(1)} %shard_map.118) | data formatting | bytes 1835008

commit v5 on v4

--- a/solution.py
+++ b/solution.py
@@ -35,7 +35,7 @@
     tokens_hbm, gain_hbm, wq_hbm, qb_hbm, wk_hbm, kb_hbm, wv_hbm, vb_hbm, wo_hbm,
     kdoc_hbm, near_hbm, far_hbm, out_ref,
     gain_ref, qb_ref, kb_ref, vb_ref, kdoc_ref, far_ref, tokens, normed, wq, wkv, wo, near, q_ref, kv_ref, kv_in, kext, acc, tops, totals, ctx, ctx_in, lent, sent, got,
-    load_sems, kv_send, kv_pass, kv_recv, kv_back, send_sem, recv_sem, ctx_send, ctx_recv, lent_send, lent_recv,
+    load_sems, kv_send, kv_pass, kv_recv, kv_back, kv_on, send_sem, recv_sem, ctx_send, ctx_recv, lent_send, lent_recv,
 ):
     place = lax.axis_index("seq")
     turn = lax.axis_index("tp")
@@ -221,48 +221,66 @@
     bent = lax.rem(place // 2, 2) == 1
     bends = reach >= 4
 
+    def kv_cut(ref, part):
+        if part == 0:
+            return ref.at[0]
+        return ref.at[1, pl.ds((part - 1) * (rows // 2), rows // 2)]
+
     def kv_copy(away, part):
         return pltpu.make_async_remote_copy(
-            src_ref=kv_ref.at[part], dst_ref=kv_in.at[away - 1, part],
-            send_sem=kv_send.at[away - 1, part], recv_sem=kv_recv.at[away - 1, part],
+            src_ref=kv_cut(kv_ref, part), dst_ref=kv_cut(kv_in.at[away - 1], part),
+            send_sem=kv_send.at[away // 2, part], recv_sem=kv_recv.at[away - 1, part],
             device_id={"seq": lax.rem(place + away, seq_count)}, device_id_type=MESH,
         )
 
     def relay(away, landing, part):
         return pltpu.make_async_remote_copy(
-            src_ref=kv_in.at[away - 1, part], dst_ref=kv_in.at[landing - 1, part],
-            send_sem=kv_pass.at[away - 1, part], recv_sem=kv_recv.at[landing - 1, part],
+            src_ref=kv_cut(kv_in.at[away - 1], part), dst_ref=kv_cut(kv_in.at[landing - 1], part),
+            send_sem=kv_pass.at[away // 2 - 1, part], recv_sem=kv_recv.at[landing - 1, part],
             device_id={"seq": partner}, device_id_type=MESH,
         )
 
     def back(part):
         return pltpu.make_async_remote_copy(
-            src_ref=kv_in.at[3, part], dst_ref=kv_in.at[1, part],
+            src_ref=kv_cut(kv_in.at[3], part), dst_ref=kv_cut(kv_in.at[1], part),
             send_sem=kv_back.at[part], recv_sem=kv_recv.at[1, part],
             device_id={"seq": lax.rem(place + seq_count - 2, seq_count)}, device_id_type=MESH,
         )
 
+    pieces = (0, 1, 2)
     evens = [away for away in range(2, reach + 2, 2) if away < seq_count]
     backs = bent & (place >= 4) & bends
+    beyond = bool(evens) and evens[-1] > reach and evens[-1] > 2
+
+    def onward(part):
+        return pltpu.make_async_remote_copy(
+            src_ref=kv_cut(kv_in.at[evens[-2] - 1], part), dst_ref=kv_cut(kv_in.at[evens[-1] - 1], part),
+            send_sem=kv_on.at[part], recv_sem=kv_recv.at[evens[-1] - 1, part],
+            device_id={"seq": lax.rem(place + 2, seq_count)}, device_id_type=MESH,
+        )
+
+    def carries(away):
+        return odd & (place >= away) & (place + 2 < seq_count)
 
     def wanted(away):
         return odd if away > reach else (place >= 0)
 
     def each_send(act):
-        for part in (0, 1):
+        for part in pieces:
             for away in evens:
                 direct = jnp.logical_not(bent & (place + 4 < seq_count) & bends & (away == 2))
 
-                @pl.when((place + away < seq_count) & wanted(away) & direct)
-                def _():
-                    act(kv_copy(away, part))
+                if not (beyond and away > reach):
+                    @pl.when((place + away < seq_count) & wanted(away) & direct)
+                    def _():
+                        act(kv_copy(away, part))
 
             @pl.when(jnp.logical_not(odd))
             def _():
                 act(kv_copy(1, part))
 
     def each_relay(act):
-        for part in (0, 1):
+        for part in pieces:
             for away in evens:
                 if away + 1 <= reach:
                     @pl.when((place >= away) & jnp.logical_not(odd))
@@ -278,8 +296,13 @@
                 def _():
                     act(back(part))
 
+            if beyond:
+                @pl.when(carries(evens[-2]))
+                def _():
+                    act(onward(part))
+
     def take(group):
-        for part in (0, 1):
+        for part in pieces:
             @pl.when(jnp.logical_not(backs & (group == 4)))
             def _():
                 kv_copy(group, part).wait_recv()
@@ -287,6 +310,12 @@
             @pl.when(odd | (group + 1 <= reach))
             def _():
                 relay(group, group + 1 - 2 * core, part).start()
+
+        if beyond:
+            @pl.when(carries(evens[-2]) & (group == evens[-2]))
+            def _():
+                for part in pieces:
+                    onward(part).start()
 
     def obtain(away):
         even = lax.rem(away, 2) == 0
@@ -306,7 +335,7 @@
 
         @pl.when(jnp.logical_not(even))
         def _():
-            for part in (0, 1):
+            for part in pieces:
                 kv_copy(away, part).wait_recv()
 
     def bounce(part):
@@ -344,17 +373,33 @@
     def sub_cut(index):
         return pl.ds(pl.multiple_of(index * sub, sub), sub)
 
+    def arrival(side, dest, index, taker):
+        half_of = taker // half
+        outward = lax.rem(side + half_of, 2)
+        near = (1 - half_of) * dest + half_of * (tp_count - 1 - dest)
+        first = (tp_count - 1 - near) * TERMS
+        second = (tp_count - 1) * TERMS + near * 2 * SUBS
+        return (1 - outward) * first + outward * second + index
+
     def term_copy(side, dest, index):
         return pltpu.make_async_remote_copy(
             src_ref=sent.at[dest, sub_cut(index)], dst_ref=got.at[side, dest, sub_cut(index)],
-            send_sem=send_sem.at[dest, index], recv_sem=recv_sem.at[side, dest, index],
+            send_sem=send_sem.at[lax.rem(dest - turn - 1 + tp_count, tp_count), index],
+            recv_sem=recv_sem.at[arrival(side, dest, index, turn + 1 - 2 * side)],
             device_id={"tp": turn + 1 - 2 * side}, device_id_type=MESH,
         )
+
+    def term_wait(side, dest, index):
+        pltpu.make_async_remote_copy(
+            src_ref=sent.at[dest, sub_cut(index)], dst_ref=got.at[side, dest, sub_cut(index)],
+            send_sem=send_sem.at[0, index], recv_sem=recv_sem.at[arrival(side, dest, index, turn)],
+            device_id={"tp": turn + 1 - 2 * side}, device_id_type=MESH,
+        ).wait_recv()
 
     def ctx_copy(index):
         return pltpu.make_async_remote_copy(
             src_ref=ctx.at[sub_cut(index)], dst_ref=ctx_in.at[sub_cut(index)],
-            send_sem=ctx_send.at[index], recv_sem=ctx_recv.at[index],
+            send_sem=ctx_send.at[index - TERMS], recv_sem=ctx_recv.at[index - TERMS],
             device_id={"tp": turn + 1 - 2 * right}, device_id_type=MESH,
         )
 
@@ -366,7 +411,7 @@
 
     def forward(side, dest, index):
         cut = sub_cut(index)
-        term_copy(side, dest, index).wait_recv()
+        term_wait(side, dest, index)
         sent[dest, cut] = (
             sent[dest, cut].astype(jnp.float32) + got[side, dest, cut].astype(jnp.float32)
         ).astype(jnp.bfloat16)
@@ -444,6 +489,7 @@
         @pl.when(part == 0)
         def _():
             bounce(1)
+            bounce(2)
 
         tail = (1 - core) * (behind // reach) * (reach % 2) if reach else 0
 
@@ -585,35 +631,6 @@
         for index in range(SUBS, 2 * SUBS):
             forward(1 - right, home, index)
 
-    @pl.loop(0, 2 * SUBS)
-    def _(index):
-        cut = sub_cut(index)
-        term_copy(1 - right, turn, index).wait_recv()
-        total = sent[turn, cut].astype(jnp.float32) + got[1 - right, turn, cut].astype(jnp.float32)
-        both = inner & (index < TERMS)
-
-        @pl.when(both)
-        def _():
-            term_copy(right, turn, index).wait_recv()
-            out_ref[cut, :] = (total + got[right, turn, cut].astype(jnp.float32)).astype(jnp.bfloat16)
-
-        @pl.when(jnp.logical_not(both))
-        def _():
-            out_ref[cut, :] = total.astype(jnp.bfloat16)
-
-    @pl.loop(0, 2 * SUBS)
-    def _(index):
-        @pl.when(inner | (index < TERMS))
-        def _():
-            for dest in range(tp_count):
-                @pl.when(dest != turn)
-                def _():
-                    term_copy(right, dest, index).wait_send()
-
-        @pl.when(outer & (index >= TERMS))
-        def _():
-            ctx_copy(index).wait_send()
-
     @pl.when(outer)
     def _():
         lend().wait_send()
@@ -622,11 +639,43 @@
     def _():
         for copy in own_spreads() + [passed_spread(index) for index in range(len(steps))]:
             copy.wait_send()
-        if len(straight) < len(steps):
+        if bent_steps:
             cross().wait_send()
 
     each_send(lambda copy: copy.wait_send())
     each_relay(lambda copy: copy.wait_send())
+
+    def finish(index):
+        cut = sub_cut(index)
+        term_wait(1 - right, turn, index)
+        total = sent[turn, cut].astype(jnp.float32) + got[1 - right, turn, cut].astype(jnp.float32)
+        both = inner & (index < TERMS)
+
+        @pl.when(both)
+        def _():
+            term_wait(right, turn, index)
+            out_ref[cut, :] = (total + got[right, turn, cut].astype(jnp.float32)).astype(jnp.bfloat16)
+
+        @pl.when(jnp.logical_not(both))
+        def _():
+            out_ref[cut, :] = total.astype(jnp.bfloat16)
+
+    @pl.loop(0, 2 * SUBS - 1)
+    def _(index):
+        finish(index)
+
+    @pl.loop(0, 2 * SUBS)
+    def _(index):
+        @pl.when(inner | (index < TERMS))
+        def _():
+            for ahead in range(1, tp_count):
+                term_copy(right, lax.rem(turn + ahead, tp_count), index).wait_send()
+
+        @pl.when(outer & (index >= TERMS))
+        def _():
+            ctx_copy(index).wait_send()
+
+    finish(2 * SUBS - 1)
 
 
 def body(
@@ -679,15 +728,16 @@
             VMEM((tp_count, rows, cols), jnp.bfloat16),
             VMEM((2, tp_count, rows, cols), jnp.bfloat16),
             pltpu.SemaphoreType.DMA((14 + spans,)),
-            pltpu.SemaphoreType.DMA((slots, 2)),
-            pltpu.SemaphoreType.DMA((slots, 2)),
-            pltpu.SemaphoreType.DMA((slots, 2)),
-            pltpu.SemaphoreType.DMA((2,)),
-            pltpu.SemaphoreType.DMA((tp_count, subs)),
-            pltpu.SemaphoreType.DMA((2, tp_count, subs)),
-            pltpu.SemaphoreType.DMA((subs,)),
-            pltpu.SemaphoreType.DMA((subs,)),
-            pltpu.SemaphoreType.DMA((2 * team,)),
+            pltpu.SemaphoreType.DMA((slots // 2 + 1, 3)),
+            pltpu.SemaphoreType.DMA((max(slots // 2, 1), 3)),
+            pltpu.SemaphoreType.DMA((slots, 3)),
+            pltpu.SemaphoreType.DMA((3,)),
+            pltpu.SemaphoreType.DMA((3,)),
+            pltpu.SemaphoreType.DMA((tp_count - 1, subs)),
+            pltpu.SemaphoreType.DMA(((tp_count - 1) * TERMS + 2 * subs,)),
+            pltpu.SemaphoreType.DMA((subs - TERMS,)),
+            pltpu.SemaphoreType.DMA((subs - TERMS,)),
+            pltpu.SemaphoreType.DMA((team,)),
             pltpu.SemaphoreType.DMA((team,)),
         ],
         compiler_params=pltpu.CompilerParams(

time: 72.8 us -> 71.7 us (0.985)
  Pallas kernels: 71.6 us -> 70.6 us
    pallas_call x1, Pallas kernels: 71.6 us -> 70.6 us  [body(): pl.pallas_call(functools.partial(attend, seq_count, tp_count, reach, chun...]
where the time goes in v5:
time: 71.7 us; the launch traced here: 71.5 us
  Pallas kernels  70.6 us (98%)
  local copies, waits for them, and re-layouts  0.93 us (1%)
    pallas_call x1, Pallas kernels, body(): pl.pallas_call(functools.partial(attend, seq_count, tp_count, reach, chun...  70.6 us

profile of v5, /device:TPU:13, one launch (start us, length us, event | category | flops | bytes accessed | tf_op | source)
XLA Modules:
  0.0 71.5 jit_solution(7538277217152002517)
XLA Ops:
  0.0 70.6 %shard_map.118 = bf16[512,896]{1,0:T(8,128)(2,1)S(1)} custom-call(bf16[512,3584]{1,0:T(8,128)(2,1)} %tokens_hbm.1, f32[3584]{0:T(1024)} %gain_hbm.1, bf16[3584,896]{1,0:T(8,128)(2,1)} %wq_hbm.1, f32[896]{0:T(1024)} %qb_hbm.1, bf16[3584,128]{1,0:T(8,128)(2,1)} %wk_hbm.1, f32[128]{0:T(128)} %kb_hbm.1, bf16[3584,128]{1,0:T(8,128)(2,1)} %wv_hbm.1, f32[128]{0:T(128)} %vb_hbm.1, ...), custom_call_target="tpu_custom_call" | custom-call | tf_op jit(solution)/shard_map/pallas_call | solution.py:700
  70.6 0.9 %copy.14 = bf16[512,896]{1,0:T(8,128)(2,1)} copy(bf16[512,896]{1,0:T(8,128)(2,1)S(1)} %shard_map.118) | data formatting | bytes 1835008

commit v6 on v5

--- a/solution.py
+++ b/solution.py
@@ -14,7 +14,7 @@
 rope_base = 1000000.0
 VMEM = pltpu.VMEM
 SUBS = 4
-TERMS = 5
+TERMS = 4
 AHEAD = 3
 BACK = 1
 

time: 71.7 us -> 71.7 us (level)
  no operation moved by 1% of the time
where the time goes in v6:
time: 71.7 us; the launch traced here: 71.5 us
  Pallas kernels  70.6 us (98%)
  local copies, waits for them, and re-layouts  0.93 us (1%)
    pallas_call x1, Pallas kernels, body(): pl.pallas_call(functools.partial(attend, seq_count, tp_count, reach, chun...  70.6 us

profile of v6, /device:TPU:13, one launch (start us, length us, event | category | flops | bytes accessed | tf_op | source)
XLA Modules:
  0.0 71.5 jit_solution(7971792238609289891)
XLA Ops:
  0.0 70.6 %shard_map.118 = bf16[512,896]{1,0:T(8,128)(2,1)S(1)} custom-call(bf16[512,3584]{1,0:T(8,128)(2,1)} %tokens_hbm.1, f32[3584]{0:T(1024)} %gain_hbm.1, bf16[3584,896]{1,0:T(8,128)(2,1)} %wq_hbm.1, f32[896]{0:T(1024)} %qb_hbm.1, bf16[3584,128]{1,0:T(8,128)(2,1)} %wk_hbm.1, f32[128]{0:T(128)} %kb_hbm.1, bf16[3584,128]{1,0:T(8,128)(2,1)} %wv_hbm.1, f32[128]{0:T(128)} %vb_hbm.1, ...), custom_call_target="tpu_custom_call" | custom-call | tf_op jit(solution)/shard_map/pallas_call | solution.py:700
  70.6 0.9 %copy.14 = bf16[512,896]{1,0:T(8,128)(2,1)} copy(bf16[512,896]{1,0:T(8,128)(2,1)S(1)} %shard_map.118) | data formatting | bytes 1835008
